TPU v7x, 256 devices: a whole 4x4x8 slice. The times are simulated.
256 devices in a mesh: expert: 16 (over x, y), tensor: 8 (over z), replica: 2 (over core).
Axes of the slice: x: 4, y: 4, z: 8, core: 2. Of those that a mesh axis runs over, the one named last changes fastest.
Arguments:
- trained: float32 [16, 7168, 2048], P('replica', 'tensor', 'expert'), may hold values from -3080 to 3080
- snapshot: bfloat16 [16, 7168, 2048], P('replica', 'tensor', 'expert'), may hold values from -3072 to 3072
- changed: int32 [16, 56, 16], P('replica', 'tensor', 'expert'), may hold values from 0 to 1, as said below
- placement: int32 [16], replicated, may hold values from 0 to 15, each once
Outputs:
- rotated_update: bfloat16 [16, 7168, 2048], P('expert', None, 'tensor')
Inputs may be any that keep to these rules, and one draw needn't show every extreme that they name: `placement`: each of the 16 experts appears exactly once. `changed`: in each aligned block of 7 block rows by 1 block columns of one expert, at most 4 entries are 1; for every expert some such block has exactly 4.
All inputs are finite; a program needn't handle non-finite values.
Results may differ from a plain program's by a relative error of at most 0.001.
Values may be sent and summed in bfloat16 or wider, within the bound.
A program may use at most 64 MiB of HBM per device.

v0:
```python
import math
import jax
import jax.numpy as jnp
from jax import lax
from jax.sharding import PartitionSpec as P

BLK = 128


def hadamard():
    positions = jnp.arange(BLK, dtype=jnp.int32)
    parity = jnp.zeros((BLK, BLK), jnp.int32)
    for bit_level in range(BLK.bit_length() - 1):
        parity = parity + (positions[:, None] >> bit_level & 1) * (
            positions[None, :] >> bit_level & 1
        )
    return (1 - 2 * (parity % 2)).astype(jnp.float32) / math.sqrt(BLK)


def body(trained, snapshot, changed, placement):
    hadamard_table = hadamard()
    local_experts, local_rows, local_cols = trained.shape
    copies = lax.axis_size("replica")
    tensor_count = lax.axis_size("tensor")
    expert_count = lax.axis_size("expert")
    members = expert_count // tensor_count
    slot_total = placement.shape[0]
    owner_slots = slot_total // expert_count
    block_rows = local_rows // BLK
    block_cols = local_cols // BLK
    part_rows = BLK // copies
    block_count = block_rows * block_cols
    capacity = (4 * block_count + 3) // 7
    block_flags = changed.reshape(local_experts, block_count)
    position = jnp.arange(block_count, dtype=jnp.int32)
    ranking = jnp.where(block_flags == 1, position[None, :], block_count + position[None, :])
    picked = jnp.argsort(ranking, axis=1)[:, :capacity]
    used_slots = jnp.take_along_axis(block_flags, picked, axis=1)
    expert_ids = jnp.arange(local_experts, dtype=jnp.int32)[:, None]
    row_ids = picked // block_cols
    col_ids = picked % block_cols
    new_tiles = trained.reshape(local_experts, block_rows, BLK, block_cols, BLK)[
        expert_ids, row_ids, :, col_ids, :
    ]
    old_tiles = snapshot.reshape(local_experts, block_rows, BLK, block_cols, BLK)[
        expert_ids, row_ids, :, col_ids, :
    ]
    delta_tiles = jnp.where(
        used_slots[:, :, None, None] == 1, new_tiles - old_tiles.astype(jnp.float32), 0.0
    )
    coded_tiles = jnp.einsum(
        "ij,pmjk->pmik", hadamard_table, delta_tiles, precision=lax.Precision.HIGHEST
    ).astype(jnp.bfloat16)
    coded_tiles = coded_tiles.reshape(local_experts, capacity, copies, part_rows, BLK)
    spots_pair = jnp.broadcast_to(picked[:, :, None], (local_experts, capacity, copies))
    tiles_all, spots_all = (
        lax.all_to_all(coded_tiles, "replica", split_axis=2, concat_axis=0, tiled=True),
        lax.all_to_all(spots_pair, "replica", split_axis=2, concat_axis=0, tiled=True),
    )
    chosen = jnp.take(tiles_all, placement, axis=0).reshape(
        slot_total, 1, 1, capacity, part_rows, BLK
    )
    chosen_spots = jnp.take(spots_all, placement, axis=0).reshape(slot_total, 1, 1, capacity)
    tiles_in, spot_numbers = (
        lax.all_to_all(
            lax.all_to_all(chosen, "expert", split_axis=0, concat_axis=2, tiled=True),
            "tensor",
            split_axis=2,
            concat_axis=1,
            tiled=True,
        ),
        lax.all_to_all(
            lax.all_to_all(chosen_spots, "expert", split_axis=0, concat_axis=2, tiled=True),
            "tensor",
            split_axis=2,
            concat_axis=1,
            tiled=True,
        ),
    )
    source_count = tiles_in.shape[1]
    one_hot = (spot_numbers[..., None] == position).astype(jnp.bfloat16)
    placed = jnp.einsum(
        "osnmg,osnmab->osngab", one_hot, tiles_in, preferred_element_type=jnp.float32
    ).astype(jnp.bfloat16)
    placed = placed.reshape(
        owner_slots, source_count, members, block_rows, block_cols, part_rows, BLK
    )
    placed = jnp.transpose(placed, (0, 1, 3, 5, 2, 4, 6))
    owner_cols = members * block_cols * BLK
    owned_rows = placed.reshape(owner_slots, source_count, block_rows, 1, part_rows, owner_cols)
    whole_rows = lax.all_gather(owned_rows, "replica", axis=3, tiled=True)
    return whole_rows.reshape(owner_slots, tensor_count * block_rows * BLK, owner_cols)


def solution(mesh):
    in_specs = (
        P("replica", "tensor", "expert"),
        P("replica", "tensor", "expert"),
        P("replica", "tensor", "expert"),
        P(),
    )
    out_specs = P("expert", None, "tensor")
    return jax.shard_map(body, mesh=mesh, in_specs=in_specs, out_specs=out_specs, check_vma=False)
```

profile of v0, /device:TPU:1, one launch (start us, length us, event | category | flops | bytes accessed | tf_op | source)
XLA Modules:
  0.0 145.1 jit_solution(11660733728816668597)
XLA Ops:
  6.5 0.9 iota_select_fusion
  8.7 6.4 %all-to-all-start = ((s32[8,4,2]{0,1,2:T(4,128)}), s32[8,4,2]{0,1,2:T(4,128)S(1)}, u32[]{:S(2)}, u32[]{:S(2)}) async-start(s32[8,4,2]{0,1,2:T(4,128)} %broadcast_in_dim.55), calls=%async_computation | async-start | bytes 8192 | tf_op jit(solution)/shard_map/all_to_all | solution.py:58
  16.4 0.8 copy.38
  18.3 0.8 gather_fusion.2
  19.1 4.0 %gather_fusion.1 = f32[32,128,128]{2,1,0:T(8,128)} fusion(f32[8,7,128,1,128]{4,2,1,0,3:T(8,128)} %bitcast.67, s32[32]{0:T(128)S(1)} %reshape.261), kind=kCustom, calls=%fused_computation.1 | custom fusion | bytes 4194688 | tf_op jit(solution)/shard_map/gather | solution.py:42
  23.2 1.9 %convert_subtract_fusion = f32[32,128,128]{2,1,0:T(8,128)S(1)} fusion(f32[32,128,128]{2,1,0:T(8,128)} %gather_fusion.1, bf16[32,128,128]{2,1,0:T(8,128)(2,1)S(1)} %gather_fusion.2), kind=kLoop, calls=%fused_computation.5 | loop fusion | flops 1048576 | bytes 5242880 | tf_op jit(solution)/shard_map/sub | solution.py:49
  25.0 2.3 %fusion.2 = bf16[8,4,128,128]{2,3,1,0:T(8,128)(2,1)S(1)} fusion(f32[8,4,128,128]{3,2,1,0:T(8,128)S(1)} %bitcast.61, pred[8,4]{1,0:T(8,128)(4,1)S(1)} %copy.48, s32[128]{0:T(128)S(1)} %get-tuple-element.7, s32[128]{0:T(128)S(1)} %get-tuple-element.8, s32[128]{0:T(128)S(1)} %get-tuple-element.9, s32[128]{0:T(128)S(1)} %get-tuple-element.10, ...), kind=kOutput, calls=%fused_computation.9 | convolution fusion | flops 806813696 | bytes 3149344 | tf_op jit(solution)/shard_map/ij,pmjk->pmik/dot_general | solution.py:51
  27.3 1.1 copy.49
  28.4 3.6 %all-to-all-start.3 = ((bf16[8,4,2,64,128]{4,3,1,0,2:T(8,128)(2,1)}), bf16[8,4,2,64,128]{4,3,1,0,2:T(8,128)(2,1)S(1)}, u32[]{:S(2)}, u32[]{:S(2)}) async-start(bf16[8,4,2,64,128]{4,3,1,0,2:T(8,128)(2,1)} %copy.49), calls=%async_computation.3 | async-start | bytes 2097152 | tf_op jit(solution)/shard_map/all_to_all | solution.py:57
  32.7 0.7 copy.43
  33.7 5.1 %all-to-all-start.1 = ((s32[16,1,1,4]{3,2,1,0:T(1,128)}), s32[16,1,1,4]{3,2,1,0:T(1,128)}, u32[]{:S(2)}, u32[]{:S(2)}) async-start(s32[16,1,1,4]{3,2,1,0:T(1,128)} %copy.43), calls=%async_computation.1 | async-start | bytes 16384 | tf_op jit(solution)/shard_map/all_to_all | solution.py:73
  38.9 2.0 %gather_fusion.3 = bf16[16,4,64,128]{3,2,1,0:T(8,128)(2,1)S(1)} fusion(bf16[16,4,64,128]{3,2,1,0:T(8,128)(2,1)} %bitcast.65, s32[1024]{0:T(1024)S(1)} %pad_clamp_fusion), kind=kCustom, calls=%fused_computation.3 | custom fusion | bytes 2097216 | tf_op jit(solution)/shard_map/jit(_take)/gather | solution.py:60
  40.8 1.1 fusion.5
  42.0 3.2 %all-to-all-done.1 = s32[16,1,1,4]{3,2,1,0:T(1,128)} async-done(((s32[16,1,1,4]{3,2,1,0:T(1,128)}), s32[16,1,1,4]{3,2,1,0:T(1,128)}, u32[]{:S(2)}, u32[]{:S(2)}) %all-to-all-start.1) | async-done | bytes 288 | tf_op jit(solution)/shard_map/all_to_all | solution.py:73
  45.2 18.6 %all_to_all.78 = bf16[16,1,1,4,64,128]{5,4,3,2,1,0:T(8,128)(2,1)S(1)} all-to-all(bf16[16,1,1,4,64,128]{5,4,3,2,1,0:T(8,128)(2,1)} %fusion.5), channel_id=1, replica_groups=mesh['expert'=16,'tensor'=8,'replica'=2] {'expert'}, dimensions={0} | all-to-all | bytes 2097152 | tf_op jit(solution)/shard_map/all_to_all | solution.py:66
  63.8 32.6 %all_to_all.79 = bf16[1,1,16,4,64,128]{5,4,3,1,0,2:T(8,128)(2,1)} all-to-all(bf16[1,1,16,4,64,128]{5,4,3,1,0,2:T(8,128)(2,1)S(1)} %bitcast.66), channel_id=1, replica_groups=mesh['expert'=16,'tensor'=8,'replica'=2] {'tensor'}, dimensions={2} | all-to-all | bytes 2097152 | tf_op jit(solution)/shard_map/all_to_all | solution.py:65
  96.3 4.3 %all-to-all-start.2 = ((s32[1,1,16,4]{3,1,0,2:T(1,128)}), s32[1,1,16,4]{3,1,0,2:T(1,128)S(1)}, u32[]{:S(2)}, u32[]{:S(2)}) async-start(s32[1,1,16,4]{3,1,0,2:T(1,128)} %bitcast.31), calls=%async_computation.2 | async-start | bytes 16384 | tf_op jit(solution)/shard_map/all_to_all | solution.py:72
  100.7 2.1 %copy.52 = bf16[1,1,16,4,64,128]{5,3,4,2,1,0:T(4,128)(2,1)S(1)} copy(bf16[1,1,16,4,64,128]{5,4,3,1,0,2:T(8,128)(2,1)} %all_to_all.79) | data formatting | bytes 2097152 | tf_op jit(solution)/shard_map/all_to_all | solution.py:65
  102.8 4.4 %all-to-all-done.2 = s32[1,1,16,4]{3,1,0,2:T(1,128)S(1)} async-done(((s32[1,1,16,4]{3,1,0,2:T(1,128)}), s32[1,1,16,4]{3,1,0,2:T(1,128)S(1)}, u32[]{:S(2)}, u32[]{:S(2)}) %all-to-all-start.2) | async-done | bytes 288 | tf_op jit(solution)/shard_map/all_to_all | solution.py:72
  107.2 1.3 convert_bitcast_fusion
  108.5 3.3 %copy.53 = bf16[1,8,7,64,2,1,128]{6,4,3,2,1,5,0:T(2,128)(2,1)} copy(bf16[1,8,7,64,2,1,128]{6,2,3,4,1,5,0:T(8,128)(2,1)S(1)} %convert_bitcast_fusion) | data formatting | bytes 3670016 | tf_op jit(solution)/shard_map/transpose | solution.py:88
  111.8 5.3 %reshape.227 = bf16[1,8,7,1,64,256]{5,4,2,1,3,0:T(8,128)(2,1)} reshape(bf16[1,8,7,64,2,1,128]{6,4,3,2,1,5,0:T(2,128)(2,1)} %copy.53) | data formatting | bytes 3670016 | tf_op jit(solution)/shard_map/reshape | solution.py:90
  117.1 16.8 %all-gather.2.cloned.1.call-done = bf16[1,8,7,2,64,256]{5,4,2,1,0,3:T(8,128)(2,1)} async-done(((bf16[1,8,7,1,64,256]{5,4,2,1,0,3:T(8,128)(2,1)}), bf16[1,8,7,2,64,256]{5,4,2,1,0,3:T(8,128)(2,1)}) %all-gather.2.cloned.1.call-update) | async-done | bytes 3670032 | tf_op jit(solution)/shard_map/all_gather | solution.py:91
  133.9 4.4 %copy.55 = bf16[1,8,7,2,64,256]{5,4,3,2,1,0:T(8,128)(2,1)} copy(bf16[1,8,7,2,64,256]{5,4,2,1,0,3:T(8,128)(2,1)} %all-gather.2.cloned.1.call-done) | data formatting | bytes 7340032 | tf_op jit(solution)/shard_map/all_gather | solution.py:91
  (32 shorter events, 4.8 us)
Async XLA Ops:
  6.5 11.8 %copy-start = (bf16[8,896,128]{2,1,0:T(8,128)(2,1)S(1)}, bf16[8,896,128]{2,1,0:T(8,128)(2,1)}, u32[]{:S(2)}) copy-start(bf16[8,896,128]{2,1,0:T(8,128)(2,1)} %param.5) | copy-start | bytes 5505028
  8.7 19.7 %all-to-all-start = ((s32[8,4,2]{0,1,2:T(4,128)}), s32[8,4,2]{0,1,2:T(4,128)S(1)}, u32[]{:S(2)}, u32[]{:S(2)}) async-start(s32[8,4,2]{0,1,2:T(4,128)} %broadcast_in_dim.55), calls=%async_computation | async-start | bytes 8192 | tf_op jit(solution)/shard_map/all_to_all | solution.py:58
  28.4 5.3 %all-to-all-start.3 = ((bf16[8,4,2,64,128]{4,3,1,0,2:T(8,128)(2,1)}), bf16[8,4,2,64,128]{4,3,1,0,2:T(8,128)(2,1)S(1)}, u32[]{:S(2)}, u32[]{:S(2)}) async-start(bf16[8,4,2,64,128]{4,3,1,0,2:T(8,128)(2,1)} %copy.49), calls=%async_computation.3 | async-start | bytes 2097152 | tf_op jit(solution)/shard_map/all_to_all | solution.py:57
  33.7 5.1 %copy-start.1 = (bf16[8,4,2,64,128]{4,3,1,0,2:T(8,128)(2,1)}, bf16[8,4,2,64,128]{4,3,1,0,2:T(8,128)(2,1)S(1)}, u32[]{:S(2)}) copy-start(bf16[8,4,2,64,128]{4,3,1,0,2:T(8,128)(2,1)S(1)} %all-to-all-done.3) | copy-start | bytes 3145732
  33.7 11.4 %all-to-all-start.1 = ((s32[16,1,1,4]{3,2,1,0:T(1,128)}), s32[16,1,1,4]{3,2,1,0:T(1,128)}, u32[]{:S(2)}, u32[]{:S(2)}) async-start(s32[16,1,1,4]{3,2,1,0:T(1,128)} %copy.43), calls=%async_computation.1 | async-start | bytes 16384 | tf_op jit(solution)/shard_map/all_to_all | solution.py:73
  96.3 10.8 %all-to-all-start.2 = ((s32[1,1,16,4]{3,1,0,2:T(1,128)}), s32[1,1,16,4]{3,1,0,2:T(1,128)S(1)}, u32[]{:S(2)}, u32[]{:S(2)}) async-start(s32[1,1,16,4]{3,1,0,2:T(1,128)} %bitcast.31), calls=%async_computation.2 | async-start | bytes 16384 | tf_op jit(solution)/shard_map/all_to_all | solution.py:72
  100.6 33.3 %all-gather.2.cloned.1.call-start = ((), (), s32[]{:S(2)}) async-start(), calls=%async_computation.6 | async-start | bytes 5505024 | tf_op jit(solution)/shard_map/all_gather | solution.py:91
Sparse Core Ops, SparseCore 0:
  117.2 16.6 all-gather.1
where the time goes:
time: 146 us; the launch traced here: 145 us
  blocking collectives  51.2 us (35%)
  local copies, waits for them, and re-layouts  26.8 us (18%)
  waiting for transfers between devices  24.8 us (17%)
  starting transfers between devices  19.4 us (13%)
  between operations  13.5 us (9%)
  other arithmetic  5.93 us (4%)
  matrix products  3.58 us (2%)
    all_to_all x1, blocking collectives, body(): lax.all_to_all(lax.all_to_all(chosen, 'expert', split_axis=0, concat_axis...  32.6 us
    all_to_all x1, blocking collectives, body(): lax.all_to_all(chosen, 'expert', split_axis=0, concat_axis=2, tiled=True)  18.6 us
    all_gather x1, waiting for transfers between devices, body(): whole_rows = lax.all_gather(owned_rows, 'replica', axis=3, tiled=True)  16.8 us
    all_to_all x1, starting transfers between devices, body(): lax.all_to_all(spots_pair, 'replica', split_axis=2, concat_axis=0, tiled=...  6.41 us
    reshape x1, local copies, waits for them, and re-layouts, body(): placed.reshape(owner_slots, source_count, block_rows, 1, part_rows, owner...  5.3 us
    all_to_all x1, starting transfers between devices, body(): lax.all_to_all(chosen_spots, 'expert', split_axis=0, concat_axis=2, tiled...  5.1 us
    all_to_all x1, waiting for transfers between devices, body(): lax.all_to_all(lax.all_to_all(chosen_spots, 'expert', split_axis=0, conca...  4.42 us
    all_gather x1, local copies, waits for them, and re-layouts, body(): whole_rows = lax.all_gather(owned_rows, 'replica', axis=3, tiled=True)  4.37 us
  transfers between devices with their start and end apart: 5, of which 4 were waited for; matrix products, arithmetic and copies ran while one was open for 14% of the time, Pallas kernels for 0%

commit v1 on v0

--- a/solution.py
+++ b/solution.py
@@ -70,7 +70,15 @@
             tiled=True,
         ),
         lax.all_to_all(
-            lax.all_to_all(chosen_spots, "expert", split_axis=0, concat_axis=2, tiled=True),
+            jnp.concatenate(
+                lax.all_to_all(
+                    jnp.stack(jnp.split(chosen_spots, lax.axis_size("expert"), axis=0)),
+                    "expert",
+                    0,
+                    0,
+                ),
+                axis=2,
+            ),
             "tensor",
             split_axis=2,
             concat_axis=1,

time: 146 us -> 155 us (1.062)
  local copies, waits for them, and re-layouts: 26.8 us -> 35.2 us
  blocking collectives: 51.2 us -> 52.8 us
    unnamed x5 -> x20, local copies, waits for them, and re-layouts: 0.77 us -> 8.91 us
  transfers between devices with their start and end apart: 5 -> 5, of which waited for: 4 -> 3; matrix products, arithmetic and copies ran while one was open for 14% -> 18% of each run, Pallas kernels for 0% -> 0%
where the time goes in v1:
time: 155 us; the launch traced here: 154 us
  blocking collectives  52.8 us (34%)
  local copies, waits for them, and re-layouts  35.2 us (23%)
  waiting for transfers between devices  24.7 us (16%)
  starting transfers between devices  18.5 us (12%)
  between operations  13.5 us (9%)
  other arithmetic  5.93 us (4%)
  matrix products  3.58 us (2%)
    all_to_all x1, blocking collectives, body(): lax.all_to_all(lax.all_to_all(chosen, 'expert', split_axis=0, concat_axis...  33.7 us
    all_to_all x1, blocking collectives, body(): lax.all_to_all(chosen, 'expert', split_axis=0, concat_axis=2, tiled=True)  19.2 us
    all_gather x1, waiting for transfers between devices, body(): whole_rows = lax.all_gather(owned_rows, 'replica', axis=3, tiled=True)  16.9 us
    unnamed x20, local copies, waits for them, and re-layouts  8.91 us
    all_to_all x1, starting transfers between devices, body(): lax.all_to_all(spots_pair, 'replica', split_axis=2, concat_axis=0, tiled=...  6.41 us
    reshape x1, local copies, waits for them, and re-layouts, body(): placed.reshape(owner_slots, source_count, block_rows, 1, part_rows, owner...  5.29 us
    all_to_all x1, starting transfers between devices, body(): lax.all_to_all(jnp.stack(jnp.split(chosen_spots, lax.axis_size('expert'),...  5.1 us
    all_to_all x1, waiting for transfers between devices, body(): lax.all_to_all(jnp.concatenate(lax.all_to_all(jnp.stack(jnp.split(chosen_...  4.41 us
  transfers between devices with their start and end apart: 5, of which 3 were waited for; matrix products, arithmetic and copies ran while one was open for 18% of the time, Pallas kernels for 0%

profile of v1, /device:TPU:1, one launch (start us, length us, event | category | flops | bytes accessed | tf_op | source)
XLA Modules:
  0.0 154.2 jit_solution(10528219385686546863)
XLA Ops:
  6.5 0.9 iota_select_fusion
  8.7 6.4 %all-to-all-start = ((s32[8,4,2]{0,1,2:T(4,128)}), s32[8,4,2]{0,1,2:T(4,128)S(1)}, u32[]{:S(2)}, u32[]{:S(2)}) async-start(s32[8,4,2]{0,1,2:T(4,128)} %broadcast_in_dim.55), calls=%async_computation | async-start | bytes 8192 | tf_op jit(solution)/shard_map/all_to_all | solution.py:58
  16.4 0.8 copy.107
  17.4 0.7 gather_fusion.4
  18.3 0.8 gather_fusion.2
  19.1 4.0 %gather_fusion.1 = f32[32,128,128]{2,1,0:T(8,128)} fusion(f32[8,7,128,1,128]{4,2,1,0,3:T(8,128)} %bitcast.99, s32[32]{0:T(128)S(1)} %reshape.290), kind=kCustom, calls=%fused_computation.1 | custom fusion | bytes 4194688 | tf_op jit(solution)/shard_map/gather | solution.py:42
  23.1 1.9 %convert_subtract_fusion = f32[32,128,128]{2,1,0:T(8,128)S(1)} fusion(f32[32,128,128]{2,1,0:T(8,128)} %gather_fusion.1, bf16[32,128,128]{2,1,0:T(8,128)(2,1)S(1)} %gather_fusion.2), kind=kLoop, calls=%fused_computation.5 | loop fusion | flops 1048576 | bytes 5242880 | tf_op jit(solution)/shard_map/sub | solution.py:49
  25.0 2.3 %fusion.2 = bf16[8,4,128,128]{2,3,1,0:T(8,128)(2,1)S(1)} fusion(f32[8,4,128,128]{3,2,1,0:T(8,128)S(1)} %bitcast.93, pred[8,4]{1,0:T(8,128)(4,1)S(1)} %copy.116, s32[128]{0:T(128)S(1)} %get-tuple-element.23, s32[128]{0:T(128)S(1)} %get-tuple-element.24, s32[128]{0:T(128)S(1)} %get-tuple-element.25, s32[128]{0:T(128)S(1)} %get-tuple-element.26, ...), kind=kOutput, calls=%fused_computation.9 | convolution fusion | flops 806813696 | bytes 3149344 | tf_op jit(solution)/shard_map/ij,pmjk->pmik/dot_general | solution.py:51
  27.3 1.1 copy.117
  28.4 3.6 %all-to-all-start.3 = ((bf16[8,4,2,64,128]{4,3,1,0,2:T(8,128)(2,1)}), bf16[8,4,2,64,128]{4,3,1,0,2:T(8,128)(2,1)S(1)}, u32[]{:S(2)}, u32[]{:S(2)}) async-start(bf16[8,4,2,64,128]{4,3,1,0,2:T(8,128)(2,1)} %copy.117), calls=%async_computation.3 | async-start | bytes 2097152 | tf_op jit(solution)/shard_map/all_to_all | solution.py:57
  41.9 5.1 %all-to-all-start.1 = ((s32[16,1,1,1,4]{4,3,2,1,0:T(1,128)}), s32[16,1,1,1,4]{4,3,2,1,0:T(1,128)}, u32[]{:S(2)}, u32[]{:S(2)}) async-start(s32[16,1,1,1,4]{4,3,2,1,0:T(1,128)} %constant_dynamic-update-slice_fusion), calls=%async_computation.1 | async-start | bytes 16384 | tf_op jit(solution)/shard_map/all_to_all | solution.py:74
  47.0 2.0 %gather_fusion.3 = bf16[16,4,64,128]{3,2,1,0:T(8,128)(2,1)S(1)} fusion(bf16[16,4,64,128]{3,2,1,0:T(8,128)(2,1)} %bitcast.97, s32[1024]{0:T(1024)S(1)} %pad_clamp_fusion), kind=kCustom, calls=%fused_computation.3 | custom fusion | bytes 2097216 | tf_op jit(solution)/shard_map/jit(_take)/gather | solution.py:60
  49.0 1.1 fusion.5
  50.1 3.4 %all-to-all-done.1 = s32[16,1,1,1,4]{4,3,2,1,0:T(1,128)} async-done(((s32[16,1,1,1,4]{4,3,2,1,0:T(1,128)}), s32[16,1,1,1,4]{4,3,2,1,0:T(1,128)}, u32[]{:S(2)}, u32[]{:S(2)}) %all-to-all-start.1) | async-done | bytes 288 | tf_op jit(solution)/shard_map/all_to_all | solution.py:74
  53.5 19.2 %all_to_all.71 = bf16[16,1,1,4,64,128]{5,4,3,2,1,0:T(8,128)(2,1)S(1)} all-to-all(bf16[16,1,1,4,64,128]{5,4,3,2,1,0:T(8,128)(2,1)} %fusion.5), channel_id=1, replica_groups=mesh['expert'=16,'tensor'=8,'replica'=2] {'expert'}, dimensions={0} | all-to-all | bytes 2097152 | tf_op jit(solution)/shard_map/all_to_all | solution.py:66
  72.6 33.7 %all_to_all.72 = bf16[1,1,16,4,64,128]{5,4,3,1,0,2:T(8,128)(2,1)} all-to-all(bf16[1,1,16,4,64,128]{5,4,3,1,0,2:T(8,128)(2,1)S(1)} %bitcast.98), channel_id=1, replica_groups=mesh['expert'=16,'tensor'=8,'replica'=2] {'tensor'}, dimensions={2} | all-to-all | bytes 2097152 | tf_op jit(solution)/shard_map/all_to_all | solution.py:65
  106.3 3.3 %all-to-all-start.2 = ((s32[1,1,16,4]{3,1,0,2:T(1,128)}), s32[1,1,16,4]{3,1,0,2:T(1,128)S(1)}, u32[]{:S(2)}, u32[]{:S(2)}) async-start(s32[1,1,16,4]{3,1,0,2:T(1,128)} %bitcast.31), calls=%async_computation.2 | async-start | bytes 16384 | tf_op jit(solution)/shard_map/all_to_all | solution.py:72
  109.7 2.1 %copy.120 = bf16[1,1,16,4,64,128]{5,3,4,2,1,0:T(4,128)(2,1)S(1)} copy(bf16[1,1,16,4,64,128]{5,4,3,1,0,2:T(8,128)(2,1)} %all_to_all.72) | data formatting | bytes 2097152 | tf_op jit(solution)/shard_map/all_to_all | solution.py:65
  111.8 4.4 %all-to-all-done.2 = s32[1,1,16,4]{3,1,0,2:T(1,128)S(1)} async-done(((s32[1,1,16,4]{3,1,0,2:T(1,128)}), s32[1,1,16,4]{3,1,0,2:T(1,128)S(1)}, u32[]{:S(2)}, u32[]{:S(2)}) %all-to-all-start.2) | async-done | bytes 288 | tf_op jit(solution)/shard_map/all_to_all | solution.py:72
  116.2 1.3 convert_bitcast_fusion
  117.5 3.3 %copy.121 = bf16[1,8,7,64,2,1,128]{6,4,3,2,1,5,0:T(2,128)(2,1)} copy(bf16[1,8,7,64,2,1,128]{6,2,3,4,1,5,0:T(8,128)(2,1)S(1)} %convert_bitcast_fusion) | data formatting | bytes 3670016 | tf_op jit(solution)/shard_map/transpose | solution.py:96
  120.8 5.3 %reshape.256 = bf16[1,8,7,1,64,256]{5,4,2,1,3,0:T(8,128)(2,1)} reshape(bf16[1,8,7,64,2,1,128]{6,4,3,2,1,5,0:T(2,128)(2,1)} %copy.121) | data formatting | bytes 3670016 | tf_op jit(solution)/shard_map/reshape | solution.py:98
  126.1 16.9 %all-gather.2.cloned.1.call-done = bf16[1,8,7,2,64,256]{5,4,2,1,0,3:T(8,128)(2,1)} async-done(((bf16[1,8,7,1,64,256]{5,4,2,1,0,3:T(8,128)(2,1)}), bf16[1,8,7,2,64,256]{5,4,2,1,0,3:T(8,128)(2,1)}) %all-gather.2.cloned.1.call-update) | async-done | bytes 3670032 | tf_op jit(solution)/shard_map/all_gather | solution.py:99
  143.0 4.4 %copy.123 = bf16[1,8,7,2,64,256]{5,4,3,2,1,0:T(8,128)(2,1)} copy(bf16[1,8,7,2,64,256]{5,4,2,1,0,3:T(8,128)(2,1)} %all-gather.2.cloned.1.call-done) | data formatting | bytes 7340032 | tf_op jit(solution)/shard_map/all_gather | solution.py:99
  (48 shorter events, 13.0 us)
Async XLA Ops:
  6.5 11.8 %copy-start = (bf16[8,896,128]{2,1,0:T(8,128)(2,1)S(1)}, bf16[8,896,128]{2,1,0:T(8,128)(2,1)}, u32[]{:S(2)}) copy-start(bf16[8,896,128]{2,1,0:T(8,128)(2,1)} %param.5) | copy-start | bytes 5505028
  8.7 19.7 %all-to-all-start = ((s32[8,4,2]{0,1,2:T(4,128)}), s32[8,4,2]{0,1,2:T(4,128)S(1)}, u32[]{:S(2)}, u32[]{:S(2)}) async-start(s32[8,4,2]{0,1,2:T(4,128)} %broadcast_in_dim.55), calls=%async_computation | async-start | bytes 8192 | tf_op jit(solution)/shard_map/all_to_all | solution.py:58
  28.4 13.5 %all-to-all-start.3 = ((bf16[8,4,2,64,128]{4,3,1,0,2:T(8,128)(2,1)}), bf16[8,4,2,64,128]{4,3,1,0,2:T(8,128)(2,1)S(1)}, u32[]{:S(2)}, u32[]{:S(2)}) async-start(bf16[8,4,2,64,128]{4,3,1,0,2:T(8,128)(2,1)} %copy.117), calls=%async_computation.3 | async-start | bytes 2097152 | tf_op jit(solution)/shard_map/all_to_all | solution.py:57
  41.9 5.1 %copy-start.1 = (bf16[8,4,2,64,128]{4,3,1,0,2:T(8,128)(2,1)}, bf16[8,4,2,64,128]{4,3,1,0,2:T(8,128)(2,1)S(1)}, u32[]{:S(2)}) copy-start(bf16[8,4,2,64,128]{4,3,1,0,2:T(8,128)(2,1)S(1)} %all-to-all-done.3) | copy-start | bytes 3145732
  41.9 11.6 %all-to-all-start.1 = ((s32[16,1,1,1,4]{4,3,2,1,0:T(1,128)}), s32[16,1,1,1,4]{4,3,2,1,0:T(1,128)}, u32[]{:S(2)}, u32[]{:S(2)}) async-start(s32[16,1,1,1,4]{4,3,2,1,0:T(1,128)} %constant_dynamic-update-slice_fusion), calls=%async_computation.1 | async-start | bytes 16384 | tf_op jit(solution)/shard_map/all_to_all | solution.py:74
  106.3 9.9 %all-to-all-start.2 = ((s32[1,1,16,4]{3,1,0,2:T(1,128)}), s32[1,1,16,4]{3,1,0,2:T(1,128)S(1)}, u32[]{:S(2)}, u32[]{:S(2)}) async-start(s32[1,1,16,4]{3,1,0,2:T(1,128)} %bitcast.31), calls=%async_computation.2 | async-start | bytes 16384 | tf_op jit(solution)/shard_map/all_to_all | solution.py:72
  109.7 33.3 %all-gather.2.cloned.1.call-start = ((), (), s32[]{:S(2)}) async-start(), calls=%async_computation.6 | async-start | bytes 5505024 | tf_op jit(solution)/shard_map/all_gather | solution.py:99
Sparse Core Ops, SparseCore 0:
  126.2 16.7 all-gather.1
